TPU v7x, 32 devices: a whole 2x2x4 slice. The times are simulated.
32 devices in a mesh: grp: 4 (over x, core), row: 4 (over z), col: 2 (over y).
Axes of the slice: x: 2, y: 2, z: 4, core: 2. Of those that a mesh axis runs over, the one named last changes fastest.
Arguments:
- cover: float32 [4, 12288, 4096], P('grp', 'row', 'col'), may hold values from -4 to 12, as said below
- prior: float32 [4096, 4096], P(('grp', 'row'), 'col'), may hold values from -0.5 to 2, as said below
Outputs:
- cover_out: float32 [4, 12288, 4096], P('grp', 'row', 'col')
- posterior: float32 [4096, 4096], P(('grp', 'row'), 'col')
Inputs may be any that keep to these rules, and one draw needn't show every extreme that they name: `cover`: the first three slots hold a symmetric positive definite matrix of order 12288 in the column-block order of the steps. `prior`: A symmetric positive definite matrix.
All inputs are finite; a program needn't handle non-finite values.
Results may differ from a plain program's by a relative error of at most 0.0001.
Values sent between devices are 32-bit elements; how exact they have to be, the bound alone decides.
No kernel may reach another device: no remote copies, remote signals or barrier semaphores. Data moves between devices by JAX's collectives and lax.ppermute only.
A program may use at most 192 MiB of HBM per device.

v0:
```python
import jax
import jax.numpy as jnp
from jax import lax
from jax.sharding import PartitionSpec as P

M = 12288
B = 256
precise = lax.Precision.HIGHEST


def broadcast(block, axis, source):
    block = jnp.where(lax.axis_index(axis) == source, block, jnp.zeros_like(block))
    return lax.psum(block, axis)


def advance(region, row_ids, block_ids, lower_rows, solved, panel, on_top):
    update = jnp.dot(lower_rows, solved, precision=precise, preferred_element_type=jnp.float32)
    to_right = block_ids > panel
    result = jnp.where((row_ids >= (panel + 1) * B) & to_right, region - update, region)
    own_column = (block_ids[:, :B] == panel) & (row_ids >= panel * B)
    result = jnp.concatenate(
        [jnp.where(own_column, lower_rows, result[:, :B]), result[:, B:]], axis=1
    )
    stripe = jnp.where(on_top & to_right, solved, result[panel * B : (panel + 1) * B])
    return jnp.concatenate([result[: panel * B], stripe, result[(panel + 1) * B :]], axis=0)


def local(cover, prior):
    local_block = cover[0]
    group_idx = lax.axis_index("grp")
    row_idx = lax.axis_index("row")
    col_idx = lax.axis_index("col")
    group_count = lax.axis_size("grp")
    row_count = lax.axis_size("row")
    col_count = lax.axis_size("col")
    local_rows, local_cols = local_block.shape
    prior_rows = prior.shape[0]
    row_ids = (row_idx * local_rows + jnp.arange(local_rows))[:, None]
    col_blocks = col_idx * (local_cols // B) + jnp.arange(local_cols) // B
    block_ids = jnp.where(
        group_idx < group_count - 1, (group_count - 1) * col_blocks + group_idx, M
    )[None, :]
    on_top = row_idx == 0
    first_col = (group_idx * row_count + row_idx) * prior_rows
    posterior = prior
    column_piece = local_block[:, :B]
    row_piece = local_block[0:B]
    panel_col = broadcast(column_piece, ("grp", "col"), 0 * col_count)
    packed = jnp.concatenate([panel_col[0:B], row_piece], axis=1)
    packed = broadcast(packed, "row", 0)
    factor = jnp.linalg.cholesky(packed[:, :B])
    lower_rows = lax.linalg.triangular_solve(
        factor, panel_col, left_side=False, lower=True, transpose_a=True
    )
    solved = lax.linalg.triangular_solve(factor, packed[:, B:], left_side=True, lower=True)
    local_block = advance(local_block, row_ids, block_ids, lower_rows, solved, 0, on_top)
    command_cols = broadcast(solved, "grp", group_count - 1)
    owner_idx = first_col // local_cols
    window = lax.dynamic_slice_in_dim(command_cols, first_col % local_cols, prior_rows, 1)
    command_rows = broadcast(window, "col", owner_idx)
    posterior = posterior - lax.dot_general(
        command_rows,
        command_cols,
        (((0,), (0,)), ((), ())),
        precision=precise,
        preferred_element_type=jnp.float32,
    )
    return (local_block[None], posterior)


def solution(mesh):
    return jax.shard_map(
        local,
        mesh=mesh,
        in_specs=(P("grp", "row", "col"), P(("grp", "row"), "col")),
        out_specs=(P("grp", "row", "col"), P(("grp", "row"), "col")),
        check_vma=False,
    )
```

profile of v0, /device:TPU:0, one launch (start us, length us, event | category | flops | bytes accessed | tf_op | source)
XLA Modules:
  0.0 432.4 jit_solution(17534666749890213730)
XLA Ops:
  7.2 24.7 %copy.4 = f32[1,3072,2048]{1,2,0:T(8,128)} copy(f32[1,3072,2048]{2,1,0:T(8,128)} %param.2) | data formatting | bytes 50331648 | tf_op args[0]
  31.9 3.9 slice_select_fusion.1
  35.9 1.7 slice_bitcast_fusion
  37.6 70.4 %all-reduce.6.cloned.1.call-done = f32[3072,256]{0,1:T(8,128)} async-done(((f32[3072,256]{0,1:T(8,128)}), f32[3072,256]{0,1:T(8,128)}) %all-reduce.6.cloned.1.call-update) | async-done | bytes 3145744 | tf_op jit(solution)/shard_map/psum | solution.py:13
  108.0 1.0 slice.107
  109.0 1.6 maximum_select_fusion
  110.8 94.6 %all-reduce.8.cloned.1.call-done = f32[256,2304]{0,1:T(8,128)} async-done(((f32[256,2304]{0,1:T(8,128)}), f32[256,2304]{0,1:T(8,128)}) %all-reduce.8.cloned.1.call-update) | async-done | bytes 2359312 | tf_op jit(solution)/shard_map/psum | solution.py:13
  205.4 1.0 slice.109
  206.5 1.0 fusion.7
  207.5 11.7 %cholesky.50 = f32[128,128]{1,0:T(8,128)S(1)} custom-call(f32[128,128]{1,0:T(8,128)S(1)} %cholesky.118), custom_call_target="Cholesky" | custom-call | tf_op jit(solution)/shard_map/jit(cholesky)/cholesky | solution.py:51
  219.3 9.8 %custom-call.16 = f32[1,128,128]{1,2,0:T(8,128)S(1)} custom-call(f32[1,128,128]{2,1,0:T(8,128)S(1)} %get-tuple-element.29), custom_call_target="InvertDiagBlocksLowerTriangular" | custom-call | tf_op jit(solution)/shard_map/jit(cholesky)/cholesky | solution.py:51
  229.6 11.7 %cholesky.105 = f32[128,128]{1,0:T(8,128)S(1)} custom-call(f32[128,128]{1,0:T(8,128)S(1)} %convolution_subtract_fusion.3), custom_call_target="Cholesky" | custom-call | tf_op jit(solution)/shard_map/jit(cholesky)/cholesky | solution.py:51
  243.7 4.2 while.1
  244.5 1.3 dynamic-slice.7
  246.5 1.3 dynamic-slice.7
  247.9 19.7 %custom-call.17 = f32[2,128,128]{1,2,0:T(8,128)S(1)} custom-call(f32[2,128,128]{2,1,0:T(8,128)S(1)} %get-tuple-element.9), custom_call_target="InvertDiagBlocksLowerTriangular" | custom-call | tf_op jit(solution)/shard_map/triangular_solve | solution.py:55
  267.6 2.3 fusion.5
  270.3 3.5 convolution_subtract_fusion.2
  273.7 1.0 fusion.12
  274.7 1.5 fusion.2
  276.3 1.6 convolution_subtract_fusion
  277.9 1.5 fusion.11
  279.4 27.7 %subtract_select_fusion = f32[3072,2048]{0,1:T(8,128)} fusion(pred[3072]{0:T(1024)(128)(4,1)S(1)} %get-tuple-element.30, pred[2048]{0:T(1024)(128)(4,1)S(1)} %get-tuple-element.32, f32[3072,128]{0,1:T(8,128)S(1)} %fusion.11, f32[3072,128]{0,1:T(8,128)S(1)} %fusion.2, f32[128,2048]{0,1:T(8,128)S(1)} %fusion.12, f32[128,2048]{0,1:T(8,128)S(1)} %copy.11, ...), kind=kOutput, calls=%fused_computation.2 | convolution fusion | flops 19347537920 | bytes 55579648 | tf_op jit(solution)/shard_map/dot_general | solution.py:17
  307.1 8.3 %slice.114 = f32[3072,1792]{0,1:T(8,128)S(1)} slice(f32[3072,2048]{0,1:T(8,128)} %subtract_select_fusion), slice={[0:3072], [256:2048]} | slice | bytes 44040192 | tf_op jit(solution)/shard_map/slice | solution.py:22
  315.4 4.9 %slice_select_fusion = f32[3072,256]{0,1:T(8,128)S(1)} fusion(f32[3072,2048]{0,1:T(8,128)} %subtract_select_fusion, f32[3072,128]{0,1:T(8,128)S(1)} %fusion.11, f32[3072,128]{0,1:T(8,128)S(1)} %fusion.2, pred[3072]{0:T(1024)(128)(4,1)S(1)} %get-tuple-element.31, pred[256]{0:T(512)(128)(4,1)S(1)} %compare_reduce_fusion), kind=kLoop, calls=%fused_computation.8 | loop fusion | flops 2359296 | bytes 9440512 | tf_op jit(solution)/shard_map/jit(_where)/select_n | solution.py:22
  320.7 3.0 fusion.4
  323.8 1.7 copy-done
  325.6 50.5 %all-reduce.10.cloned.1.call-done = f32[256,2048]{0,1:T(8,128)} async-done(((f32[256,2048]{0,1:T(8,128)}), f32[256,2048]{0,1:T(8,128)}) %all-reduce.10.cloned.1.call-update) | async-done | bytes 2097168 | tf_op jit(solution)/shard_map/psum | solution.py:13
  376.0 1.7 dynamic-slice_select_fusion
  377.7 18.3 %fusion.1 = f32[1,3072,2048]{1,2,0:T(8,128)} fusion(f32[3072,1792]{0,1:T(8,128)} %copy-done, f32[3072,256]{0,1:T(8,128)S(1)} %slice_select_fusion, f32[256,2048]{0,1:T(8,128)} %get-tuple-element.27), kind=kLoop, calls=%fused_computation.5 | loop fusion | flops 31457280 | bytes 52428800 | tf_op jit(solution)/shard_map/broadcast_in_dim | solution.py:68
  396.0 24.9 %copy.13 = f32[1,3072,2048]{2,1,0:T(8,128)} copy(f32[1,3072,2048]{1,2,0:T(8,128)} %fusion.1) | data formatting | bytes 50331648
  420.9 4.9 %convolution_subtract_fusion.1 = f32[256,2048]{1,0:T(8,128)} fusion(f32[256,2048]{1,0:T(8,128)} %param.3, f32[256,256]{0,1:T(8,128)} %all-reduce.12.cloned.1.call-done, f32[256,2048]{0,1:T(8,128)S(1)} %copy-done.4), kind=kOutput, calls=%fused_computation.11 | convolution fusion | flops 1611137024 | bytes 6553600 | tf_op jit(solution)/shard_map/dot_general | solution.py:61
  (49 shorter events, 4.2 us)
Async XLA Ops:
  7.2 100.9 %all-reduce.6.cloned.1.call-start = ((), (), s32[]{:S(2)}) async-start(), calls=%async_computation | async-start | bytes 6291456 | tf_op jit(solution)/shard_map/psum | solution.py:13
  35.8 169.6 %all-reduce.8.cloned.1.call-start = ((), (), s32[]{:S(2)}) async-start(), calls=%async_computation.1 | async-start | bytes 4718592 | tf_op jit(solution)/shard_map/psum | solution.py:13
  110.6 265.5 %all-reduce.10.cloned.1.call-start = ((), (), s32[]{:S(2)}) async-start(), calls=%async_computation.2 | async-start | bytes 4194304 | tf_op jit(solution)/shard_map/psum | solution.py:13
  270.2 9.2 %copy-start.1 = (f32[128,2048]{0,1:T(8,128)}, f32[128,2048]{0,1:T(8,128)S(1)}, u32[]{:S(2)}) copy-start(f32[128,2048]{0,1:T(8,128)S(1)} %copy.11) | copy-start | bytes 3145732
  270.3 4.5 %copy-start.3 = (f32[3072,256]{0,1:T(8,128)S(1)}, f32[3072,256]{0,1:T(8,128)}, u32[]{:S(2)}) copy-start(f32[3072,256]{0,1:T(8,128)} %all-reduce.6.cloned.1.call-done) | copy-start | bytes 9437188
  315.4 10.1 %copy-start = (f32[3072,1792]{0,1:T(8,128)}, f32[3072,1792]{0,1:T(8,128)S(1)}, u32[]{:S(2)}) copy-start(f32[3072,1792]{0,1:T(8,128)S(1)} %slice.114) | copy-start | bytes 66060292
  315.4 5.3 %copy-start.2 = (f32[128,2048]{0,1:T(8,128)S(1)}, f32[128,2048]{0,1:T(8,128)}, u32[]{:S(2)}) copy-start(f32[128,2048]{0,1:T(8,128)} %copy-done.1) | copy-start | bytes 3145732
  325.5 95.4 %all-reduce.12.cloned.1.call-start = ((), (), s32[]{:S(2)}) async-start(), calls=%async_computation.3 | async-start | bytes 524288 | tf_op jit(solution)/shard_map/psum | solution.py:13
  396.0 24.9 %copy-start.4 = (f32[256,2048]{0,1:T(8,128)S(1)}, f32[256,2048]{0,1:T(8,128)}, u32[]{:S(2)}) copy-start(f32[256,2048]{0,1:T(8,128)} %all-reduce.10.cloned.1.call-done) | copy-start | bytes 6291460
Sparse Core Ops, SparseCore 0:
  36.0 72.0 all-reduce.5
  110.7 94.6 all-reduce.7
  325.6 50.3 all-reduce.9
  378.7 23.3 all-reduce.11
where the time goes:
time: 433 us; the launch traced here: 432 us
  waiting for transfers between devices  216 us (50%)
  other arithmetic  88.2 us (20%)
  local copies, waits for them, and re-layouts  68.4 us (16%)
  matrix products  44.5 us (10%)
  between operations  15.3 us (4%)
    psum x4, waiting for transfers between devices, broadcast(): return lax.psum(block, axis)  215 us
    unnamed x12, local copies, waits for them, and re-layouts  51.6 us
    another operation x6, other arithmetic, local(): factor = jnp.linalg.cholesky(packed[:, :B])  34 us
    dot_general x1, matrix products, advance(): jnp.dot(lower_rows, solved, precision=precise, preferred_element_type=jnp...  27.7 us
    another operation x3, other arithmetic, local(): lax.linalg.triangular_solve(factor, packed[:, B:], left_side=True, lower=...  19.7 us
    broadcast_in_dim x1, other arithmetic, local(): return (local_block[None], posterior)  18.3 us
    select_n x4, other arithmetic, broadcast(): jnp.where(lax.axis_index(axis) == source, block, jnp.zeros_like(block))  10.2 us
  transfers between devices with their start and end apart: 4, of which 3 were waited for; matrix products, arithmetic and copies ran while one was open for 10% of the time, Pallas kernels for 0%

commit v1 on v0

--- a/solution.py
+++ b/solution.py
@@ -10,7 +10,7 @@
 
 def broadcast(block, axis, source):
     block = jnp.where(lax.axis_index(axis) == source, block, jnp.zeros_like(block))
-    return lax.psum(block, axis)
+    return jnp.sum(lax.all_gather(block, axis), axis=0)
 
 
 def advance(region, row_ids, block_ids, lower_rows, solved, panel, on_top):

time: 433 us -> 481 us (1.11)
  waiting for transfers between devices: 216 us -> 292 us
  local copies, waits for them, and re-layouts: 68.4 us -> 19.6 us
  blocking collectives: 0 us -> 8.97 us
  other arithmetic: 88.2 us -> 95.4 us
    all_gather x0 -> x3, waiting for transfers between devices: none -> 292 us  [broadcast(): return jnp.sum(lax.all_gather(block, axis), axis=0)]
    psum x4 -> x0, waiting for transfers between devices: 215 us -> none  [broadcast(): return lax.psum(block, axis)]
    unnamed x12 -> x7, local copies, waits for them, and re-layouts: 51.6 us -> 0.83 us
    reduce_sum x0 -> x4, other arithmetic: none -> 18.5 us  [broadcast(): return jnp.sum(lax.all_gather(block, axis), axis=0)]
    all_gather x0 -> x1, blocking collectives: none -> 8.97 us  [broadcast(): return jnp.sum(lax.all_gather(block, axis), axis=0)]
    broadcast_in_dim x1, other arithmetic: 18.3 us -> 10.3 us  [local(): return (local_block[None], posterior)]
    another operation x3, matrix products: 4.66 us -> 10.7 us  [local(): lax.linalg.triangular_solve(factor, panel_col, left_side=False, lower=Tru...]
  transfers between devices with their start and end apart: 4 -> 3, of which waited for: 3 -> 2; matrix products, arithmetic and copies ran while one was open for 10% -> 14% of each run, Pallas kernels for 0% -> 0%
where the time goes in v1:
time: 481 us; the launch traced here: 480 us
  waiting for transfers between devices  292 us (61%)
  other arithmetic  95.4 us (20%)
  matrix products  48.7 us (10%)
  local copies, waits for them, and re-layouts  19.6 us (4%)
  between operations  15.3 us (3%)
  blocking collectives  8.97 us (2%)
    all_gather x3, waiting for transfers between devices, broadcast(): return jnp.sum(lax.all_gather(block, axis), axis=0)  292 us
    another operation x6, other arithmetic, local(): factor = jnp.linalg.cholesky(packed[:, :B])  34 us
    dot_general x1, matrix products, advance(): jnp.dot(lower_rows, solved, precision=precise, preferred_element_type=jnp...  28.7 us
    another operation x3, other arithmetic, local(): lax.linalg.triangular_solve(factor, packed[:, B:], left_side=True, lower=...  19.7 us
    reduce_sum x4, other arithmetic, broadcast(): return jnp.sum(lax.all_gather(block, axis), axis=0)  18.5 us
    another operation x3, matrix products, local(): lax.linalg.triangular_solve(factor, panel_col, left_side=False, lower=Tru...  10.7 us
    broadcast_in_dim x1, other arithmetic, local(): return (local_block[None], posterior)  10.3 us
  transfers between devices with their start and end apart: 3, of which 2 were waited for; matrix products, arithmetic and copies ran while one was open for 14% of the time, Pallas kernels for 0%

profile of v1, /device:TPU:0, one launch (start us, length us, event | category | flops | bytes accessed | tf_op | source)
XLA Modules:
  0.0 480.0 jit_solution(11029405899571831227)
XLA Ops:
  7.2 3.8 slice_select_fusion.1
  11.1 3.1 slice.85
  14.2 124.9 %all-gather.10.cloned.1.call-done = f32[24576,256]{1,0:T(8,128)} async-done(((f32[3072,256]{1,0:T(8,128)}), f32[24576,256]{1,0:T(8,128)}) %all-gather.10.cloned.1.call-update) | async-done | bytes 25165840 | tf_op jit(solution)/shard_map/all_gather | solution.py:13
  139.1 9.5 %reduce_sum.36 = f32[3072,256]{1,0:T(8,128)S(1)} reduce(f32[8,3072,256]{2,1,0:T(8,128)} %bitcast.49, f32[]{:T(128)} %constant.150.clone.1), dimensions={0}, to_apply=%region_0.1 | reduce | flops 5505024 | bytes 28311556 | tf_op jit(solution)/shard_map/reduce_sum | solution.py:13
  148.6 4.3 maximum_select_fusion
  153.0 166.8 %all-gather.6.cloned.1.call-done = f32[4,256,2304]{2,1,0:T(8,128)} async-done(((f32[1,256,2304]{2,1,0:T(8,128)}), f32[4,256,2304]{2,1,0:T(8,128)}) %all-gather.6.cloned.1.call-update) | async-done | bytes 9437200 | tf_op jit(solution)/shard_map/all_gather | solution.py:13
  319.8 4.5 reduce_sum.37
  324.6 11.7 %cholesky.50 = f32[128,128]{1,0:T(8,128)S(1)} custom-call(f32[128,128]{1,0:T(8,128)S(1)} %cholesky.118), custom_call_target="Cholesky" | custom-call | tf_op jit(solution)/shard_map/jit(cholesky)/cholesky | solution.py:51
  336.3 9.8 %custom-call.16 = f32[1,128,128]{1,2,0:T(8,128)S(1)} custom-call(f32[1,128,128]{2,1,0:T(8,128)S(1)} %get-tuple-element.23), custom_call_target="InvertDiagBlocksLowerTriangular" | custom-call | tf_op jit(solution)/shard_map/jit(cholesky)/cholesky | solution.py:51
  346.6 11.7 %cholesky.105 = f32[128,128]{1,0:T(8,128)S(1)} custom-call(f32[128,128]{1,0:T(8,128)S(1)} %convolution_subtract_fusion.3), custom_call_target="Cholesky" | custom-call | tf_op jit(solution)/shard_map/jit(cholesky)/cholesky | solution.py:51
  358.4 0.7 compare_reduce_fusion.1
  360.5 4.2 while.1
  360.6 0.7 fusion.38
  361.3 1.3 bitcast_dynamic-update-slice_fusion.2
  363.3 1.3 bitcast_dynamic-update-slice_fusion.2
  364.7 0.7 copy-done.2
  365.4 19.7 %custom-call.17 = f32[2,128,128]{1,2,0:T(8,128)S(1)} custom-call(f32[2,128,128]{2,1,0:T(8,128)S(1)} %get-tuple-element.9), custom_call_target="InvertDiagBlocksLowerTriangular" | custom-call | tf_op jit(solution)/shard_map/triangular_solve | solution.py:55
  385.0 1.0 fusion.4
  386.1 1.9 convolution_subtract_fusion.2
  388.0 1.1 fusion.11
  389.0 1.5 maximum_select_fusion.2
  390.7 4.2 fusion.2
  394.8 3.2 copy.10
  398.1 5.1 %convolution_subtract_fusion = f32[3072,128]{1,0:T(8,128)S(1)} fusion(f32[3072,128]{0,1:T(8,128)} %fusion.2, f32[3072,256]{1,0:T(8,128)} %copy-done.1, f32[256,256]{1,0:T(8,128)} %copy-done.2), kind=kOutput, calls=%fused_computation.7 | convolution fusion | flops 604372992 | bytes 4784128 | tf_op jit(solution)/shard_map/triangular_solve | solution.py:52
  403.2 1.4 fusion.10
  404.7 28.7 %subtract_select_fusion = f32[3072,2048]{1,0:T(8,128)} fusion(pred[2048]{0:T(1024)(128)(4,1)S(1)} %fusion.20, pred[3072]{0:T(1024)(128)(4,1)S(1)} %get-tuple-element.26, f32[3072,128]{1,0:T(8,128)S(1)} %fusion.10, f32[3072,128]{1,0:T(8,128)S(1)} %copy-done, f32[128,2048]{1,0:T(8,128)S(1)} %fusion.11, f32[128,2048]{1,0:T(8,128)S(1)} %fusion.4, ...), kind=kOutput, calls=%fused_computation.2 | convolution fusion | flops 19347537920 | bytes 55579648 | tf_op jit(solution)/shard_map/dot_general | solution.py:17
  433.3 8.3 %slice.110 = f32[3072,1792]{1,0:T(8,128)S(1)} slice(f32[3072,2048]{1,0:T(8,128)} %subtract_select_fusion), slice={[0:3072], [256:2048]} | slice | bytes 44040192 | tf_op jit(solution)/shard_map/slice | solution.py:22
  441.6 3.0 slice_select_fusion
  444.9 10.3 %fusion.1 = f32[1,3072,2048]{2,1,0:T(8,128)} fusion(f32[3072,1792]{1,0:T(8,128)S(1)} %slice.110, f32[3072,256]{1,0:T(8,128)S(1)} %slice_select_fusion, f32[256,2048]{1,0:T(8,128)S(1)} %maximum_select_fusion.1), kind=kLoop, calls=%fused_computation.5 | loop fusion | flops 31457280 | bytes 52428800 | tf_op jit(solution)/shard_map/broadcast_in_dim | solution.py:68
  455.2 4.4 reduce_sum.38
  459.6 9.0 %all-gather.1 = f32[512,256]{1,0:T(8,128)S(1)} all-gather(f32[256,256]{1,0:T(8,128)S(1)} %dynamic-slice_select_fusion), channel_id=3, replica_groups=mesh['grp'=4,'row'=4,'col'=2] {'col'}, dimensions={0}, use_global_device_ids=true | all-gather | bytes 786432 | tf_op jit(solution)/shard_map/all_gather | solution.py:13
  468.6 4.8 %convolution_subtract_fusion.1 = f32[256,2048]{1,0:T(8,128)} fusion(f32[256,2048]{1,0:T(8,128)} %param.3, f32[256,256]{1,0:T(8,128)S(1)} %reduce_sum.39, f32[256,2048]{1,0:T(8,128)S(1)} %reduce_sum.38), kind=kOutput, calls=%fused_computation.11 | convolution fusion | flops 1611137024 | bytes 6553600 | tf_op jit(solution)/shard_map/dot_general | solution.py:61
  (38 shorter events, 2.2 us)
Async XLA Ops:
  7.2 131.9 %all-gather.10.cloned.1.call-start = ((), (), s32[]{:S(2)}) async-start(), calls=%async_computation.2 | async-start | bytes 28311552 | tf_op jit(solution)/shard_map/all_gather | solution.py:13
  11.0 308.8 %all-gather.6.cloned.1.call-start = ((), (), s32[]{:S(2)}) async-start(), calls=%async_computation | async-start | bytes 11796480 | tf_op jit(solution)/shard_map/all_gather | solution.py:13
  148.6 4.3 copy-start.1
  152.9 302.3 %all-gather.8.cloned.1.call-start = ((), (), s32[]{:S(2)}) async-start(), calls=%async_computation.1 | async-start | bytes 10485760 | tf_op jit(solution)/shard_map/all_gather | solution.py:13
  364.7 0.7 copy-start.2
  403.2 1.5 copy-start
Sparse Core Ops, SparseCore 0:
  11.1 127.9 all-gather.9
  153.0 166.7 all-gather.5
  390.6 56.4 all-gather.7
